TPU v7x, 768 devices: a whole 4x8x12 slice. The times are simulated.
768 devices in a mesh: dom: 48 (over y_hi, z, core), grp: 16 (over x, y_lo).
Axes of the slice: x: 4, y: 8 (y_hi: 2, y_lo: 4; y = y_hi * 4 + y_lo), z: 12, core: 2. Of those that a mesh axis runs over, the one named last changes fastest.
Arguments:
- fine_level_residual: float32 [3, 15, 98304], P(None, None, ('dom', 'grp')), may hold values from -6 to 6
- restriction_matrix: float32 [3, 15], replicated, may hold values from -1.5 to 1.5
- prolongation_matrix: float32 [15, 3], replicated, may hold values from -3.5 to 3.5
- block_inverse: bfloat16 [9, 9, 98304], P(None, None, 'dom')
- face_coupling: bfloat16 [3, 9, 9, 98304], P(None, None, None, 'dom'), may hold values from -1.75 to 1.75
- neighbours: int32 [3, 98304], P(None, 'dom'), may hold values from -2048 to 2048, as said below
Outputs:
- correction: float32 [3, 15, 98304], P(None, None, ('dom', 'grp'))
Inputs may be any that keep to these rules, and one draw needn't show every extreme that they name: `neighbours`: each entry is 0 or a nonzero offset d with |d| at most 2048 such that e + d is another triangle of the grid.
All inputs are finite; a program needn't handle non-finite values.
Results may differ from a plain program's by a relative error of at most 0.0003.
Values sent between devices are 32-bit elements; how exact they have to be, the bound alone decides.
A program may use at most 32 MiB of HBM per device.

v0:
```python
import jax
import jax.numpy as jnp
from jax import lax
from jax.sharding import PartitionSpec as P

SWEEPS = 6


damping = 0.8


def sent_to_all(shard, axis):
    copies = jnp.broadcast_to(shard, (lax.axis_size(axis), *shard.shape))
    return lax.all_to_all(copies, axis, split_axis=0, concat_axis=0, tiled=True)


def laid_out(parts, dim):
    dims = list(parts.shape[1:])
    dims[dim] *= parts.shape[0]
    return jnp.moveaxis(parts, 0, dim).reshape(dims)


def collect(shard, axis, dim):
    parts = sent_to_all(shard, axis)
    return laid_out(parts, dim)


def extended_2(block, sides, width):
    for axis, dim in sides:
        count = lax.axis_size(axis)
        forward = [(i, i + 1) for i in range(count - 1)]
        backward = [(target, source) for source, target in forward]
        low = lax.ppermute(
            lax.slice_in_dim(block, block.shape[dim] - width, None, axis=dim), axis, forward
        )
        high = lax.ppermute(lax.slice_in_dim(block, 0, width, axis=dim), axis, backward)
        block = jnp.concatenate([low, block, high], axis=dim)
    return block


def apply_inverse(block_inverse, remain):
    return jnp.sum(block_inverse.astype(jnp.float32) * remain[None, :, :], axis=1)


def later_sweep(
    current_iterate, coarse_forcing, block_inverse, face_coupling, neighbours, extended, anchor
):
    coupled = jnp.zeros_like(current_iterate)
    length = extended.shape[1]
    columns = jnp.arange(current_iterate.shape[1], dtype=jnp.int32)
    for face_index in range(3):
        offsets = neighbours[face_index]
        position = jnp.clip(columns + offsets + anchor, 0, length - 1)
        present = (offsets != 0).astype(jnp.float32)
        beside = extended[:, position] * present[None, :]
        coupled = coupled + jnp.sum(
            face_coupling[face_index].astype(jnp.float32) * beside[None, :, :], axis=1
        )
    update = apply_inverse(block_inverse, coarse_forcing - coupled)
    return (1.0 - damping) * current_iterate + damping * update


def local(
    fine_level_residual,
    restriction_matrix,
    prolongation_matrix,
    block_inverse,
    face_coupling,
    neighbours,
):
    element_width = fine_level_residual.shape[2]
    block_width = block_inverse.shape[2]
    local_rhs = jnp.einsum(
        "oc,acw->aow", restriction_matrix, fine_level_residual, precision=lax.Precision.HIGHEST
    )
    local_rhs = local_rhs.reshape(9, element_width)
    start = lax.axis_index("grp") * element_width
    inverse_part = lax.dynamic_slice_in_dim(block_inverse, start, element_width, 2)
    coupling_part = lax.dynamic_slice_in_dim(face_coupling, start, element_width, 3)
    neighbour_part = lax.dynamic_slice_in_dim(neighbours, start, element_width, 1)
    current_iterate = damping * apply_inverse(inverse_part, local_rhs)
    for sweep_index in range(1, SWEEPS):
        gathered = collect(current_iterate, "grp", 1)
        extended = extended_2(gathered, (("dom", 1),), block_width)
        current_iterate = later_sweep(
            current_iterate,
            local_rhs,
            inverse_part,
            coupling_part,
            neighbour_part,
            extended,
            block_width + start,
        )
    return jnp.einsum(
        "oc,dcz->doz",
        prolongation_matrix,
        current_iterate.reshape(3, 3, element_width),
        precision=lax.Precision.HIGHEST,
    )


def solution(mesh):
    placed = (
        P(None, None, ("dom", "grp")),
        P(),
        P(),
        P(None, None, "dom"),
        P(None, None, None, "dom"),
        P(None, "dom"),
    )
    return jax.shard_map(
        local, mesh=mesh, in_specs=placed, out_specs=P(None, None, ("dom", "grp")), check_vma=False
    )
```

profile of v0, /device:TPU:56, one launch (start us, length us, event | category | flops | bytes accessed | tf_op | source)
XLA Modules:
  0.0 182.2 jit_solution(8058106139145137685)
XLA Ops:
  0.0 0.9 convolution_bitcast_fusion.1
  0.9 0.8 fusion.15
  1.7 0.6 broadcast_in_dim.10
  2.4 7.6 %all-to-all-start = ((f32[16,9,128]{2,1,0:T(8,128)}), f32[16,9,128]{2,1,0:T(8,128)S(1)}, u32[]{:S(2)}, u32[]{:S(2)}) async-start(f32[16,9,128]{2,1,0:T(8,128)} %broadcast_in_dim.10), calls=%async_computation | async-start | bytes 262144 | tf_op jit(solution)/shard_map/all_to_all | solution.py:14
  10.0 1.2 constant_dynamic-slice_fusion
  11.3 4.2 %all-to-all-done = f32[16,9,128]{2,1,0:T(8,128)S(1)} async-done(((f32[16,9,128]{2,1,0:T(8,128)}), f32[16,9,128]{2,1,0:T(8,128)S(1)}, u32[]{:S(2)}, u32[]{:S(2)}) %all-to-all-start) | async-done | bytes 73760 | tf_op jit(solution)/shard_map/all_to_all | solution.py:14
  15.5 14.9 %collective-permute-start.1 = (f32[9,2048]{1,0:T(8,128)S(1)}, f32[9,2048]{1,0:T(8,128)S(1)}, u32[]{:S(2)}, u32[]{:S(2)}) collective-permute-start(f32[9,2048]{1,0:T(8,128)S(1)} %bitcast.147), channel_id=1, source_target_pairs={{16,0},{32,16},{48,32},{64,48},{80,64},{96,80},{112,96},{128,112},... | collective-permute-start | bytes 221192 | tf_op jit(solution)/shard_map/ppermute | solution.py:36
  30.5 1.9 %collective-permute-start = (f32[9,2048]{1,0:T(8,128)S(1)}, f32[9,2048]{1,0:T(8,128)S(1)}, u32[]{:S(2)}, u32[]{:S(2)}) collective-permute-start(f32[9,2048]{1,0:T(8,128)S(1)} %bitcast.148), channel_id=1, source_target_pairs={{0,16},{16,32},{32,48},{48,64},{64,80},{80,96},{96,112},{112,128},... | collective-permute-start | bytes 221192 | tf_op jit(solution)/shard_map/ppermute | solution.py:33
  32.4 0.5 collective-permute-done.1
  33.0 11.2 %collective-permute-done = f32[9,2048]{1,0:T(8,128)S(1)} collective-permute-done((f32[9,2048]{1,0:T(8,128)S(1)}, f32[9,2048]{1,0:T(8,128)S(1)}, u32[]{:S(2)}, u32[]{:S(2)}) %collective-permute-start) | collective-permute-done | bytes 73760 | tf_op jit(solution)/shard_map/ppermute | solution.py:33
  44.2 0.8 pad_maximum_fusion
  44.9 1.9 %copy.81 = f32[9,6144]{0,1:T(8,128)S(1)} copy(f32[9,6144]{1,0:T(8,128)} %pad_maximum_fusion) | data formatting | bytes 442368 | tf_op jit(solution)/shard_map/concatenate | solution.py:37
  46.9 0.6 gather_fusion.2
  47.7 0.7 gather_fusion.1
  48.3 0.6 gather_fusion
  49.1 0.1 multiply_bitcast_fusion.13
  49.4 0.8 fusion.16
  50.2 11.1 %all_to_all.25 = f32[16,9,128]{2,1,0:T(8,128)S(1)} all-to-all(f32[16,9,128]{2,1,0:T(8,128)S(1)} %broadcast_in_dim.11), channel_id=1, replica_groups=mesh['dom'=48,'grp'=16] {'grp'}, dimensions={0} | all-to-all | bytes 147456 | tf_op jit(solution)/shard_map/all_to_all | solution.py:14
  61.5 1.9 %collective-permute-start.3 = (f32[9,2048]{1,0:T(8,128)S(1)}, f32[9,2048]{1,0:T(8,128)S(1)}, u32[]{:S(2)}, u32[]{:S(2)}) collective-permute-start(f32[9,2048]{1,0:T(8,128)S(1)} %bitcast.150), channel_id=1, source_target_pairs={{16,0},{32,16},{48,32},{64,48},{80,64},{96,80},{112,96},{128,112},... | collective-permute-start | bytes 221192 | tf_op jit(solution)/shard_map/ppermute | solution.py:36
  63.4 2.4 %collective-permute-start.2 = (f32[9,2048]{1,0:T(8,128)S(1)}, f32[9,2048]{1,0:T(8,128)S(1)}, u32[]{:S(2)}, u32[]{:S(2)}) collective-permute-start(f32[9,2048]{1,0:T(8,128)S(1)} %bitcast.151), channel_id=1, source_target_pairs={{0,16},{16,32},{32,48},{48,64},{64,80},{80,96},{96,112},{112,128},... | collective-permute-start | bytes 221192 | tf_op jit(solution)/shard_map/ppermute | solution.py:33
  65.8 0.1 collective-permute-done.3
  65.9 11.1 %collective-permute-done.2 = f32[9,2048]{1,0:T(8,128)S(1)} collective-permute-done((f32[9,2048]{1,0:T(8,128)S(1)}, f32[9,2048]{1,0:T(8,128)S(1)}, u32[]{:S(2)}, u32[]{:S(2)}) %collective-permute-start.2) | collective-permute-done | bytes 73760 | tf_op jit(solution)/shard_map/ppermute | solution.py:33
  77.0 0.8 pad_maximum_fusion.1
  77.7 1.9 %copy.88 = f32[9,6144]{0,1:T(8,128)S(1)} copy(f32[9,6144]{1,0:T(8,128)} %pad_maximum_fusion.1) | data formatting | bytes 442368 | tf_op jit(solution)/shard_map/concatenate | solution.py:37
  79.7 0.6 gather_fusion.5
  80.3 0.6 gather_fusion.4
  81.0 0.6 gather_fusion.3
  81.8 0.1 multiply_bitcast_fusion.11
  82.2 0.8 fusion.17
  83.1 10.8 %all_to_all.26 = f32[16,9,128]{2,1,0:T(8,128)S(1)} all-to-all(f32[16,9,128]{2,1,0:T(8,128)S(1)} %broadcast_in_dim.12), channel_id=1, replica_groups=mesh['dom'=48,'grp'=16] {'grp'}, dimensions={0} | all-to-all | bytes 147456 | tf_op jit(solution)/shard_map/all_to_all | solution.py:14
  93.9 1.9 %collective-permute-start.5 = (f32[9,2048]{1,0:T(8,128)S(1)}, f32[9,2048]{1,0:T(8,128)S(1)}, u32[]{:S(2)}, u32[]{:S(2)}) collective-permute-start(f32[9,2048]{1,0:T(8,128)S(1)} %bitcast.153), channel_id=1, source_target_pairs={{16,0},{32,16},{48,32},{64,48},{80,64},{96,80},{112,96},{128,112},... | collective-permute-start | bytes 221192 | tf_op jit(solution)/shard_map/ppermute | solution.py:36
  95.9 2.4 %collective-permute-start.4 = (f32[9,2048]{1,0:T(8,128)S(1)}, f32[9,2048]{1,0:T(8,128)S(1)}, u32[]{:S(2)}, u32[]{:S(2)}) collective-permute-start(f32[9,2048]{1,0:T(8,128)S(1)} %bitcast.154), channel_id=1, source_target_pairs={{0,16},{16,32},{32,48},{48,64},{64,80},{80,96},{96,112},{112,128},... | collective-permute-start | bytes 221192 | tf_op jit(solution)/shard_map/ppermute | solution.py:33
  98.3 0.1 collective-permute-done.5
  98.4 11.1 %collective-permute-done.4 = f32[9,2048]{1,0:T(8,128)S(1)} collective-permute-done((f32[9,2048]{1,0:T(8,128)S(1)}, f32[9,2048]{1,0:T(8,128)S(1)}, u32[]{:S(2)}, u32[]{:S(2)}) %collective-permute-start.4) | collective-permute-done | bytes 73760 | tf_op jit(solution)/shard_map/ppermute | solution.py:33
  109.5 0.8 pad_maximum_fusion.2
  110.2 1.9 %copy.95 = f32[9,6144]{0,1:T(8,128)S(1)} copy(f32[9,6144]{1,0:T(8,128)} %pad_maximum_fusion.2) | data formatting | bytes 442368 | tf_op jit(solution)/shard_map/concatenate | solution.py:37
  112.2 0.6 gather_fusion.8
  112.8 0.6 gather_fusion.7
  113.5 0.8 gather_fusion.6
  114.4 0.1 multiply_bitcast_fusion.8
  114.8 0.8 fusion.18
  115.7 10.8 %all_to_all.27 = f32[16,9,128]{2,1,0:T(8,128)S(1)} all-to-all(f32[16,9,128]{2,1,0:T(8,128)S(1)} %broadcast_in_dim.13), channel_id=1, replica_groups=mesh['dom'=48,'grp'=16] {'grp'}, dimensions={0} | all-to-all | bytes 147456 | tf_op jit(solution)/shard_map/all_to_all | solution.py:14
  126.6 1.9 %collective-permute-start.7 = (f32[9,2048]{1,0:T(8,128)S(1)}, f32[9,2048]{1,0:T(8,128)S(1)}, u32[]{:S(2)}, u32[]{:S(2)}) collective-permute-start(f32[9,2048]{1,0:T(8,128)S(1)} %bitcast.156), channel_id=1, source_target_pairs={{16,0},{32,16},{48,32},{64,48},{80,64},{96,80},{112,96},{128,112},... | collective-permute-start | bytes 221192 | tf_op jit(solution)/shard_map/ppermute | solution.py:36
  128.5 2.4 %collective-permute-start.6 = (f32[9,2048]{1,0:T(8,128)S(1)}, f32[9,2048]{1,0:T(8,128)S(1)}, u32[]{:S(2)}, u32[]{:S(2)}) collective-permute-start(f32[9,2048]{1,0:T(8,128)S(1)} %bitcast.157), channel_id=1, source_target_pairs={{0,16},{16,32},{32,48},{48,64},{64,80},{80,96},{96,112},{112,128},... | collective-permute-start | bytes 221192 | tf_op jit(solution)/shard_map/ppermute | solution.py:33
  130.9 0.1 collective-permute-done.7
  131.0 11.1 %collective-permute-done.6 = f32[9,2048]{1,0:T(8,128)S(1)} collective-permute-done((f32[9,2048]{1,0:T(8,128)S(1)}, f32[9,2048]{1,0:T(8,128)S(1)}, u32[]{:S(2)}, u32[]{:S(2)}) %collective-permute-start.6) | collective-permute-done | bytes 73760 | tf_op jit(solution)/shard_map/ppermute | solution.py:33
  142.1 0.8 pad_maximum_fusion.3
  142.8 1.9 %copy.102 = f32[9,6144]{0,1:T(8,128)S(1)} copy(f32[9,6144]{1,0:T(8,128)} %pad_maximum_fusion.3) | data formatting | bytes 442368 | tf_op jit(solution)/shard_map/concatenate | solution.py:37
  144.8 0.8 gather_fusion.11
  145.6 0.8 gather_fusion.10
  146.3 0.8 gather_fusion.9
  147.7 0.8 fusion.19
  148.5 10.8 %all_to_all.28 = f32[16,9,128]{2,1,0:T(8,128)S(1)} all-to-all(f32[16,9,128]{2,1,0:T(8,128)S(1)} %broadcast_in_dim.14), channel_id=1, replica_groups=mesh['dom'=48,'grp'=16] {'grp'}, dimensions={0} | all-to-all | bytes 147456 | tf_op jit(solution)/shard_map/all_to_all | solution.py:14
  159.4 1.9 %collective-permute-start.9 = (f32[9,2048]{1,0:T(8,128)S(1)}, f32[9,2048]{1,0:T(8,128)S(1)}, u32[]{:S(2)}, u32[]{:S(2)}) collective-permute-start(f32[9,2048]{1,0:T(8,128)S(1)} %bitcast.159), channel_id=1, source_target_pairs={{16,0},{32,16},{48,32},{64,48},{80,64},{96,80},{112,96},{128,112},... | collective-permute-start | bytes 221192 | tf_op jit(solution)/shard_map/ppermute | solution.py:36
  161.4 2.4 %collective-permute-start.8 = (f32[9,2048]{1,0:T(8,128)S(1)}, f32[9,2048]{1,0:T(8,128)S(1)}, u32[]{:S(2)}, u32[]{:S(2)}) collective-permute-start(f32[9,2048]{1,0:T(8,128)S(1)} %bitcast.160), channel_id=1, source_target_pairs={{0,16},{16,32},{32,48},{48,64},{64,80},{80,96},{96,112},{112,128},... | collective-permute-start | bytes 221192 | tf_op jit(solution)/shard_map/ppermute | solution.py:33
  163.8 0.1 collective-permute-done.9
  163.9 11.1 %collective-permute-done.8 = f32[9,2048]{1,0:T(8,128)S(1)} collective-permute-done((f32[9,2048]{1,0:T(8,128)S(1)}, f32[9,2048]{1,0:T(8,128)S(1)}, u32[]{:S(2)}, u32[]{:S(2)}) %collective-permute-start.8) | collective-permute-done | bytes 73760 | tf_op jit(solution)/shard_map/ppermute | solution.py:33
  174.9 0.8 pad_maximum_fusion.4
  175.7 1.9 %copy.109 = f32[9,6144]{0,1:T(8,128)S(1)} copy(f32[9,6144]{1,0:T(8,128)} %pad_maximum_fusion.4) | data formatting | bytes 442368 | tf_op jit(solution)/shard_map/concatenate | solution.py:37
  177.6 0.8 gather_fusion.14
  178.4 0.8 gather_fusion.13
  179.2 0.8 gather_fusion.12
  180.6 0.8 fusion.20
  181.4 0.8 convolution_bitcast_fusion
  (89 shorter events, 3.1 us)
Async XLA Ops:
  0.0 9.9 %copy-start = (s32[3,2048]{1,0:T(4,128)S(1)}, s32[3,2048]{1,0:T(4,128)}, u32[]{:S(2)}) copy-start(s32[3,2048]{1,0:T(4,128)} %param.11) | copy-start | bytes 73732
  2.4 13.1 %all-to-all-start = ((f32[16,9,128]{2,1,0:T(8,128)}), f32[16,9,128]{2,1,0:T(8,128)S(1)}, u32[]{:S(2)}, u32[]{:S(2)}) async-start(f32[16,9,128]{2,1,0:T(8,128)} %broadcast_in_dim.10), calls=%async_computation | async-start | bytes 262144 | tf_op jit(solution)/shard_map/all_to_all | solution.py:14
  10.0 102.2 %copy-start.2 = (s32[1024]{0:T(1024)}, s32[1024]{0:T(1024)S(1)}, u32[]{:S(2)}) copy-start(s32[1024]{0:T(1024)S(1)} %get-tuple-element.14) | copy-start | bytes 12292
  10.0 102.8 %copy-start.1 = (s32[1024]{0:T(1024)}, s32[1024]{0:T(1024)S(1)}, u32[]{:S(2)}) copy-start(s32[1024]{0:T(1024)S(1)} %get-tuple-element.15) | copy-start | bytes 12292
  15.5 17.4 %collective-permute-start.1 = (f32[9,2048]{1,0:T(8,128)S(1)}, f32[9,2048]{1,0:T(8,128)S(1)}, u32[]{:S(2)}, u32[]{:S(2)}) collective-permute-start(f32[9,2048]{1,0:T(8,128)S(1)} %bitcast.147), channel_id=1, source_target_pairs={{16,0},{32,16},{48,32},{64,48},{80,64},{96,80},{112,96},{128,112},... | collective-permute-start | bytes 221192 | tf_op jit(solution)/shard_map/ppermute | solution.py:36
  30.5 13.7 %collective-permute-start = (f32[9,2048]{1,0:T(8,128)S(1)}, f32[9,2048]{1,0:T(8,128)S(1)}, u32[]{:S(2)}, u32[]{:S(2)}) collective-permute-start(f32[9,2048]{1,0:T(8,128)S(1)} %bitcast.148), channel_id=1, source_target_pairs={{0,16},{16,32},{32,48},{48,64},{64,80},{80,96},{96,112},{112,128},... | collective-permute-start | bytes 221192 | tf_op jit(solution)/shard_map/ppermute | solution.py:33
  32.4 48.6 %copy-start.3 = (s32[1024]{0:T(1024)}, s32[1024]{0:T(1024)S(1)}, u32[]{:S(2)}) copy-start(s32[1024]{0:T(1024)S(1)} %pad_clamp_fusion.2) | copy-start | bytes 12292
  61.5 4.4 %collective-permute-start.3 = (f32[9,2048]{1,0:T(8,128)S(1)}, f32[9,2048]{1,0:T(8,128)S(1)}, u32[]{:S(2)}, u32[]{:S(2)}) collective-permute-start(f32[9,2048]{1,0:T(8,128)S(1)} %bitcast.150), channel_id=1, source_target_pairs={{16,0},{32,16},{48,32},{64,48},{80,64},{96,80},{112,96},{128,112},... | collective-permute-start | bytes 221192 | tf_op jit(solution)/shard_map/ppermute | solution.py:36
  63.4 13.6 %collective-permute-start.2 = (f32[9,2048]{1,0:T(8,128)S(1)}, f32[9,2048]{1,0:T(8,128)S(1)}, u32[]{:S(2)}, u32[]{:S(2)}) collective-permute-start(f32[9,2048]{1,0:T(8,128)S(1)} %bitcast.151), channel_id=1, source_target_pairs={{0,16},{16,32},{32,48},{48,64},{64,80},{80,96},{96,112},{112,128},... | collective-permute-start | bytes 221192 | tf_op jit(solution)/shard_map/ppermute | solution.py:33
  93.9 4.4 %collective-permute-start.5 = (f32[9,2048]{1,0:T(8,128)S(1)}, f32[9,2048]{1,0:T(8,128)S(1)}, u32[]{:S(2)}, u32[]{:S(2)}) collective-permute-start(f32[9,2048]{1,0:T(8,128)S(1)} %bitcast.153), channel_id=1, source_target_pairs={{16,0},{32,16},{48,32},{64,48},{80,64},{96,80},{112,96},{128,112},... | collective-permute-start | bytes 221192 | tf_op jit(solution)/shard_map/ppermute | solution.py:36
  95.9 13.6 %collective-permute-start.4 = (f32[9,2048]{1,0:T(8,128)S(1)}, f32[9,2048]{1,0:T(8,128)S(1)}, u32[]{:S(2)}, u32[]{:S(2)}) collective-permute-start(f32[9,2048]{1,0:T(8,128)S(1)} %bitcast.154), channel_id=1, source_target_pairs={{0,16},{16,32},{32,48},{48,64},{64,80},{80,96},{96,112},{112,128},... | collective-permute-start | bytes 221192 | tf_op jit(solution)/shard_map/ppermute | solution.py:33
  126.6 4.4 %collective-permute-start.7 = (f32[9,2048]{1,0:T(8,128)S(1)}, f32[9,2048]{1,0:T(8,128)S(1)}, u32[]{:S(2)}, u32[]{:S(2)}) collective-permute-start(f32[9,2048]{1,0:T(8,128)S(1)} %bitcast.156), channel_id=1, source_target_pairs={{16,0},{32,16},{48,32},{64,48},{80,64},{96,80},{112,96},{128,112},... | collective-permute-start | bytes 221192 | tf_op jit(solution)/shard_map/ppermute | solution.py:36
  128.5 13.6 %collective-permute-start.6 = (f32[9,2048]{1,0:T(8,128)S(1)}, f32[9,2048]{1,0:T(8,128)S(1)}, u32[]{:S(2)}, u32[]{:S(2)}) collective-permute-start(f32[9,2048]{1,0:T(8,128)S(1)} %bitcast.157), channel_id=1, source_target_pairs={{0,16},{16,32},{32,48},{48,64},{64,80},{80,96},{96,112},{112,128},... | collective-permute-start | bytes 221192 | tf_op jit(solution)/shard_map/ppermute | solution.py:33
  148.5 32.9 %copy-start.4 = (f32[15,3]{0,1:T(4,128)S(1)}, f32[15,3]{0,1:T(4,128)}, u32[]{:S(2)}) copy-start(f32[15,3]{0,1:T(4,128)} %param.8) | copy-start | bytes 544
  159.4 4.4 %collective-permute-start.9 = (f32[9,2048]{1,0:T(8,128)S(1)}, f32[9,2048]{1,0:T(8,128)S(1)}, u32[]{:S(2)}, u32[]{:S(2)}) collective-permute-start(f32[9,2048]{1,0:T(8,128)S(1)} %bitcast.159), channel_id=1, source_target_pairs={{16,0},{32,16},{48,32},{64,48},{80,64},{96,80},{112,96},{128,112},... | collective-permute-start | bytes 221192 | tf_op jit(solution)/shard_map/ppermute | solution.py:36
  161.4 13.6 %collective-permute-start.8 = (f32[9,2048]{1,0:T(8,128)S(1)}, f32[9,2048]{1,0:T(8,128)S(1)}, u32[]{:S(2)}, u32[]{:S(2)}) collective-permute-start(f32[9,2048]{1,0:T(8,128)S(1)} %bitcast.160), channel_id=1, source_target_pairs={{0,16},{16,32},{32,48},{48,64},{64,80},{80,96},{96,112},{112,128},... | collective-permute-start | bytes 221192 | tf_op jit(solution)/shard_map/ppermute | solution.py:33
where the time goes:
time: 183 us; the launch traced here: 182 us
  waiting for transfers between devices  60.6 us (33%)
  blocking collectives  43.5 us (24%)
  starting transfers between devices  41.7 us (23%)
  local copies, waits for them, and re-layouts  23.5 us (13%)
  other arithmetic  10.5 us (6%)
    ppermute x5, waiting for transfers between devices, extended_2(): lax.ppermute(lax.slice_in_dim(block, block.shape[dim] - width, None, axis...  55.6 us
    all_to_all x4, blocking collectives, sent_to_all(): return lax.all_to_all(copies, axis, split_axis=0, concat_axis=0, tiled=True)  43.5 us
    ppermute x5, starting transfers between devices, extended_2(): lax.ppermute(lax.slice_in_dim(block, 0, width, axis=dim), axis, backward)  22.6 us
    ppermute x5, starting transfers between devices, extended_2(): lax.ppermute(lax.slice_in_dim(block, block.shape[dim] - width, None, axis...  11.5 us
    gather x15, local copies, waits for them, and re-layouts, later_sweep(): beside = extended[:, position] * present[None, :]  10.5 us
    concatenate x5, local copies, waits for them, and re-layouts, extended_2(): block = jnp.concatenate([low, block, high], axis=dim)  9.63 us
    all_to_all x1, starting transfers between devices, sent_to_all(): return lax.all_to_all(copies, axis, split_axis=0, concat_axis=0, tiled=True)  7.57 us
    reduce_sum x6, other arithmetic, apply_inverse(): jnp.sum(block_inverse.astype(jnp.float32) * remain[None, :, :], axis=1)  4.79 us
  transfers between devices with their start and end apart: 11, of which 11 were waited for; matrix products, arithmetic and copies ran while one was open for 1% of the time, Pallas kernels for 0%

commit v1 on v0

v1 whole, which is shorter than its diff:
```python
import jax
import jax.numpy as jnp
from jax import lax
from jax.experimental import pallas as pl
from jax.experimental.pallas import tpu as pltpu
from jax.sharding import PartitionSpec as P

SWEEPS = 6
MESH = pl.DeviceIdType.MESH
damping = 0.8
N_GRP = 16
LANES = 128


def gathered(x, lane):
    return jnp.take_along_axis(x, lane, axis=1, mode="promise_in_bounds")


def kernel(
    n_dom,
    res_ref,
    rmat_ref,
    nb_ref,
    inv_hbm,
    cpl_hbm,
    out_ref,
    inv_v,
    cpl_v,
    dense,
    lane_idx,
    block_idx,
    own_rhs,
    land,
    rhs,
    table,
    beside,
    load_sem,
    gsend,
    grecv,
    hsend,
    hrecv,
):
    d = lax.axis_index("dom")
    g = lax.axis_index("grp")
    half = n_dom // 2
    mirror = (g // 4) * 4 + (3 - g % 4)
    low_g = jnp.where(d == half, mirror, g)
    high_g = jnp.where(d == half - 1, mirror, g)
    has_low = d > 0
    has_high = d < n_dom - 1

    barrier = pltpu.get_barrier_semaphore()
    for step in range(1, N_GRP):
        peer = lax.rem(g + step, N_GRP)
        pl.semaphore_signal(barrier, inc=1, device_id=(d, peer), device_id_type=MESH)

    @pl.when(has_low)
    def _():
        pl.semaphore_signal(barrier, inc=1, device_id=(d - 1, low_g), device_id_type=MESH)

    @pl.when(has_high)
    def _():
        pl.semaphore_signal(barrier, inc=1, device_id=(d + 1, high_g), device_id_type=MESH)

    load_inv = pltpu.make_async_copy(inv_hbm, inv_v, load_sem.at[0])
    load_cpl = pltpu.make_async_copy(cpl_hbm, cpl_v, load_sem.at[1])
    load_inv.start()
    load_cpl.start()

    for m in range(3):
        total = jnp.zeros((3, LANES), jnp.float32)
        for n in range(15):
            total = total + rmat_ref[m, n] * res_ref[:, n, :]
        for v in range(3):
            own_rhs[3 * v + m : 3 * v + m + 1, :] = total[v : v + 1, :]

    for f in range(3):
        for b in range(N_GRP):
            lane_idx[f, b : b + 1, :] = nb_ref[f : f + 1, b * LANES : (b + 1) * LANES]
        offsets = lane_idx[f]
        lanes = lax.broadcasted_iota(jnp.int32, (N_GRP, LANES), 1)
        column = offsets + lanes + N_GRP * LANES
        block_idx[f] = jnp.where(offsets != 0, lax.shift_right_arithmetic(column, 7), -1)
        lane_idx[f] = jnp.bitwise_and(column, LANES - 1)

    signals = N_GRP - 1 + has_low.astype(jnp.int32) + has_high.astype(jnp.int32)
    pl.semaphore_wait(barrier, signals)

    def rhs_copy(peer, source):
        return pltpu.make_async_remote_copy(
            src_ref=own_rhs,
            dst_ref=land.at[source],
            send_sem=gsend.at[peer],
            recv_sem=grecv.at[source],
            device_id=(d, peer),
            device_id_type=MESH,
        )

    for step in range(1, N_GRP):
        peer = lax.rem(g + step, N_GRP)
        rhs_copy(peer, g).start()

    load_inv.wait()

    def spread_inv(i, carry):
        for b in range(N_GRP):
            tile = inv_v[i, :, b * LANES : (b + 1) * LANES].astype(jnp.float32)
            dense[pl.ds(i * 144 + b, 9, stride=16), :] = tile
        return carry

    lax.fori_loop(0, 9, spread_inv, 0)
    load_cpl.wait()

    def spread_cpl(ij, carry):
        for b in range(N_GRP):
            tile = cpl_v[ij, :, b * LANES : (b + 1) * LANES].astype(jnp.float32)
            dense[pl.ds(1296 + ij * 16 + b, 3, stride=1296), :] = tile
        return carry

    lax.fori_loop(0, 81, spread_cpl, 0)

    land[g] = own_rhs[...]
    for step in range(1, N_GRP):
        peer = lax.rem(g + step, N_GRP)
        rhs_copy(peer, peer).wait_recv()
    for b in range(N_GRP):
        rhs[pl.ds(b, 9, stride=16), :] = land[b]

    def matrix(base, i, j, half_index):
        start = (base + i) * 144 + j * 16 + half_index * 8
        return dense[start : start + 8, :]

    def apply_inverse(remain, half_index):
        result = []
        for i in range(9):
            total = matrix(0, i, 0, half_index) * remain[0]
            for j in range(1, 9):
                total = total + matrix(0, i, j, half_index) * remain[j]
            result.append(total)
        return result

    for h in range(2):
        remain = [rhs[j * 16 + h * 8 : j * 16 + h * 8 + 8, :] for j in range(9)]
        for i, update in enumerate(apply_inverse(remain, h)):
            table[0, i, 16 + 8 * h : 24 + 8 * h, :] = damping * update

    def to_low(slot):
        return pltpu.make_async_remote_copy(
            src_ref=table.at[slot, :, 16:32, :],
            dst_ref=table.at[slot, :, 32:48, :],
            send_sem=hsend.at[slot, 0],
            recv_sem=hrecv.at[slot, 1],
            device_id=(d - 1, low_g),
            device_id_type=MESH,
        )

    def to_high(slot):
        return pltpu.make_async_remote_copy(
            src_ref=table.at[slot, :, 16:32, :],
            dst_ref=table.at[slot, :, 0:16, :],
            send_sem=hsend.at[slot, 1],
            recv_sem=hrecv.at[slot, 0],
            device_id=(d + 1, high_g),
            device_id_type=MESH,
        )

    def send(slot):
        @pl.when(has_low)
        def _():
            to_low(slot).start()

        @pl.when(has_high)
        def _():
            to_high(slot).start()

    send(0)

    def pick(slot, h, ks, resume):
        for f in range(3):
            lane = lane_idx[f, 8 * h : 8 * h + 8, :]
            block = block_idx[f, 8 * h : 8 * h + 8, :]
            masks = [block == k for k in ks]
            for v in range(9):
                if resume:
                    total = beside[f * 9 + v, 8 * h : 8 * h + 8, :]
                else:
                    total = jnp.zeros((8, LANES), jnp.float32)
                for k, mask in zip(ks, masks):
                    source = table[slot, v, 8 * h + k : 8 * h + k + 8, :]
                    total = jnp.where(mask, gathered(source, lane), total)
                beside[f * 9 + v, 8 * h : 8 * h + 8, :] = total

    def sweep(slot, carry):
        for h in range(2):
            pick(slot, h, range(16 - 8 * h, 25 - 8 * h), False)

        @pl.when(has_low)
        def _():
            to_high(slot).wait_recv()

        @pl.when(has_high)
        def _():
            to_low(slot).wait_recv()

        for h in range(2):
            ks = [k for k in range(33) if k < 16 - 8 * h or k >= 25 - 8 * h]
            pick(slot, h, ks, True)
            near = [beside[n, 8 * h : 8 * h + 8, :] for n in range(27)]
            remain = []
            for i in range(9):
                total = jnp.zeros((8, LANES), jnp.float32)
                for f in range(3):
                    for j in range(9):
                        total = total + matrix(9 + 9 * f, i, j, h) * near[9 * f + j]
                remain.append(rhs[i * 16 + h * 8 : i * 16 + h * 8 + 8, :] - total)
            for i, update in enumerate(apply_inverse(remain, h)):
                now = table[slot, i, 16 + 8 * h : 24 + 8 * h, :]
                table[slot + 1, i, 16 + 8 * h : 24 + 8 * h, :] = (
                    1.0 - damping
                ) * now + damping * update

        @pl.when(slot < SWEEPS - 2)
        def _():
            send(slot + 1)

        return carry

    lax.fori_loop(0, SWEEPS - 1, sweep, 0)

    for i in range(9):
        out_ref[i : i + 1, :] = table[SWEEPS - 1, i, pl.ds(16 + g, 1), :]

    for step in range(1, N_GRP):
        peer = lax.rem(g + step, N_GRP)
        rhs_copy(peer, g).wait_send()
    for slot in range(SWEEPS - 1):

        @pl.when(has_low)
        def _():
            to_low(slot).wait_send()

        @pl.when(has_high)
        def _():
            to_high(slot).wait_send()


def solution(mesh):
    n_dom = mesh.shape["dom"]

    def local(
        fine_level_residual,
        restriction_matrix,
        prolongation_matrix,
        block_inverse,
        face_coupling,
        neighbours,
    ):
        width = block_inverse.shape[2]
        call = pl.pallas_call(
            lambda *refs: kernel(n_dom, *refs),
            out_shape=jax.ShapeDtypeStruct((9, LANES), jnp.float32),
            in_specs=[
                pl.BlockSpec(memory_space=pltpu.VMEM),
                pl.BlockSpec(memory_space=pltpu.SMEM),
                pl.BlockSpec(memory_space=pltpu.VMEM),
                pl.BlockSpec(memory_space=pl.ANY),
                pl.BlockSpec(memory_space=pl.ANY),
            ],
            out_specs=pl.BlockSpec(memory_space=pltpu.VMEM),
            scratch_shapes=[
                pltpu.VMEM((9, 9, width), jnp.bfloat16),
                pltpu.VMEM((81, 3, width), jnp.bfloat16),
                pltpu.VMEM((36 * 144, LANES), jnp.float32),
                pltpu.VMEM((3, 16, LANES), jnp.int32),
                pltpu.VMEM((3, 16, LANES), jnp.int32),
                pltpu.VMEM((9, LANES), jnp.float32),
                pltpu.VMEM((16, 9, LANES), jnp.float32),
                pltpu.VMEM((144, LANES), jnp.float32),
                pltpu.VMEM((SWEEPS, 9, 48, LANES), jnp.float32),
                pltpu.VMEM((27, 16, LANES), jnp.float32),
                pltpu.SemaphoreType.DMA((2,)),
                pltpu.SemaphoreType.DMA((16,)),
                pltpu.SemaphoreType.DMA((16,)),
                pltpu.SemaphoreType.DMA((SWEEPS - 1, 2)),
                pltpu.SemaphoreType.DMA((SWEEPS - 1, 2)),
            ],
            compiler_params=pltpu.CompilerParams(collective_id=0, has_side_effects=True),
            name="jacobi",
        )
        iterate = call(
            fine_level_residual,
            restriction_matrix,
            neighbours,
            block_inverse,
            face_coupling.transpose(1, 2, 0, 3).reshape(81, 3, width),
        )
        parts = iterate.reshape(3, 3, LANES)
        return sum(
            prolongation_matrix[None, :, m, None] * parts[:, None, m, :] for m in range(3)
        )

    placed = (
        P(None, None, ("dom", "grp")),
        P(),
        P(),
        P(None, None, "dom"),
        P(None, None, None, "dom"),
        P(None, "dom"),
    )
    return jax.shard_map(
        local, mesh=mesh, in_specs=placed, out_specs=P(None, None, ("dom", "grp")), check_vma=False
    )
```

time: 183 us -> 58.1 us (0.32)
  the two profiles are of different devices: /device:TPU:56 before, /device:TPU:40 now
where the time goes in v1:
time: 58.1 us; the launch traced here: 57.8 us
  Pallas kernels  55.6 us (96%)
  local copies, waits for them, and re-layouts  1.51 us (3%)
  other arithmetic  0.69 us (1%)
    pallas_call x1, Pallas kernels, local(): call(fine_level_residual, restriction_matrix, neighbours, block_inverse,...  55.6 us

profile of v1, /device:TPU:40, one launch (start us, length us, event | category | flops | bytes accessed | tf_op | source)
XLA Modules:
  0.0 57.8 jit_solution(6414821199119736123)
XLA Ops:
  0.0 0.8 %slice_bitcast_fusion.2 = (f32[15]{0:T(128)S(1)}, f32[15]{0:T(128)S(1)}, f32[15]{0:T(128)S(1)}) fusion(f32[15,3]{0,1:T(4,128)} %param.8), kind=kLoop, calls=%fused_computation.6 | loop fusion | bytes 360 | tf_op jit(solution)/shard_map/mul | solution.py:299
  0.8 55.6 %jacobi.1 = f32[9,128]{1,0:T(8,128)} custom-call(f32[3,15,128]{2,1,0:T(8,128)} %refs_0_.1, f32[3,15]{1,0:T(4,128)} %refs_1_.1, s32[3,2048]{1,0:T(4,128)} %refs_2_.1, bf16[9,9,2048]{2,1,0:T(8,128)(2,1)} %refs_3_.1, bf16[81,3,2048]{2,1,0:T(4,128)(2,1)} %bitcast.16), custom_call_target="tpu_custom_call" | custom-call | tf_op jit(solution)/shard_map/jacobi/pallas_call | solution.py:290
  56.4 0.7 %reshape.10 = f32[3,3,128]{2,1,0:T(4,128)S(1)} reshape(f32[9,128]{1,0:T(8,128)} %jacobi.1) | data formatting | bytes 9216 | tf_op jit(solution)/shard_map/reshape | solution.py:297
  57.1 0.7 %multiply_add_fusion = f32[3,15,128]{2,1,0:T(8,128)} fusion(f32[3,128]{1,0:T(4,128)S(1)} %get-tuple-element.11, f32[15]{0:T(128)S(1)} %get-tuple-element.9, f32[3,128]{1,0:T(4,128)S(1)} %get-tuple-element.12, f32[15]{0:T(128)S(1)} %get-tuple-element.10, f32[3,128]{1,0:T(4,128)S(1)} %bitcast.17, f32[15]{0:T(128)S(1)} %get-tuple-element.8), kind=kLoop, calls=%fused_computation | loop fusion | flops 28800 | bytes 27828 | tf_op jit(solution)/shard_map/add | solution.py:298
  (3 shorter events, 0.0 us)

commit v2 on v1

v2 whole, which is shorter than its diff:
```python
import jax
import jax.numpy as jnp
from jax import lax
from jax.experimental import pallas as pl
from jax.experimental.pallas import tpu as pltpu
from jax.sharding import PartitionSpec as P

SWEEPS = 6
MESH = pl.DeviceIdType.MESH
damping = 0.8
N_GRP = 16
LANES = 128


def gathered(x, lane):
    return jnp.take_along_axis(x, lane, axis=1, mode="promise_in_bounds")


def kernel(
    n_dom,
    res_hbm,
    rmat_hbm,
    pmat_hbm,
    nb_hbm,
    inv_hbm,
    cpl_hbm,
    out_ref,
    res_ref,
    rmat_ref,
    pmat_ref,
    nb_ref,
    inv_v,
    cpl_v,
    dense,
    lane_idx,
    block_idx,
    own_rhs,
    land,
    rhs,
    table,
    beside,
    final,
    load_sem,
    gsend,
    grecv,
    hsend,
    hrecv,
):
    d = lax.axis_index("dom")
    g = lax.axis_index("grp")
    half = n_dom // 2
    column, row = g // 4 * 4, g % 4
    lead = jnp.logical_or(row == 0, row == 3)
    cross_low, cross_high = d == half, d == half - 1
    has = (d > 0, d < n_dom - 1)
    cross = (cross_low, cross_high)
    first_row = 3 - row
    second_row = jnp.where(row == 3, 1, 2)
    source_row = jnp.where(row < 2, 3, 0)
    side_dom = (d - 1, d + 1)
    first = [jnp.where(cross[s], column + first_row, g) for s in range(2)]
    second = column + second_row
    source = [jnp.where(cross[s], column + source_row, g) for s in range(2)]
    sends = [
        jnp.logical_and(has[s], jnp.logical_or(jnp.logical_not(cross[s]), lead)) for s in range(2)
    ]
    twice = [jnp.logical_and(cross[s], lead) for s in range(2)]

    barrier = pltpu.get_barrier_semaphore()
    for step in range(1, N_GRP):
        peer = lax.rem(g + step, N_GRP)
        pl.semaphore_signal(barrier, inc=1, device_id=(d, peer), device_id_type=MESH)
    for s in range(2):

        @pl.when(has[s])
        def _():
            pl.semaphore_signal(
                barrier, inc=1, device_id=(side_dom[s], source[s]), device_id_type=MESH
            )

    loads = [
        pltpu.make_async_copy(src, dst, load_sem.at[i])
        for i, (src, dst) in enumerate(
            (
                (res_hbm, res_ref),
                (rmat_hbm, rmat_ref),
                (pmat_hbm, pmat_ref),
                (nb_hbm, nb_ref),
                (inv_hbm, inv_v),
                (cpl_hbm, cpl_v),
            )
        )
    ]
    for load in loads:
        load.start()

    loads[0].wait()
    loads[1].wait()
    for m in range(3):
        total = jnp.zeros((3, LANES), jnp.float32)
        for n in range(15):
            total = total + rmat_ref[m, n] * res_ref[:, n, :]
        for v in range(3):
            own_rhs[3 * v + m : 3 * v + m + 1, :] = total[v : v + 1, :]

    signals = N_GRP - 1
    for flag in sends + twice:
        signals = signals + flag.astype(jnp.int32)
    pl.semaphore_wait(barrier, signals)

    def rhs_copy(peer, owner):
        return pltpu.make_async_remote_copy(
            src_ref=own_rhs,
            dst_ref=land.at[owner],
            send_sem=gsend.at[peer],
            recv_sem=grecv.at[owner],
            device_id=(d, peer),
            device_id_type=MESH,
        )

    for step in range(1, N_GRP):
        peer = lax.rem(g + step, N_GRP)
        rhs_copy(peer, g).start()

    loads[2].wait()
    loads[3].wait()
    for f in range(3):
        for b in range(N_GRP):
            lane_idx[f, b : b + 1, :] = nb_ref[f : f + 1, b * LANES : (b + 1) * LANES]
        offsets = lane_idx[f]
        lanes = lax.broadcasted_iota(jnp.int32, (N_GRP, LANES), 1)
        position = offsets + lanes + N_GRP * LANES
        block_idx[f] = jnp.where(offsets != 0, lax.shift_right_arithmetic(position, 7), -1)
        lane_idx[f] = jnp.bitwise_and(position, LANES - 1)

    loads[4].wait()

    def spread_inv(i, carry):
        for b in range(N_GRP):
            tile = inv_v[i, :, b * LANES : (b + 1) * LANES].astype(jnp.float32)
            dense[pl.ds(i * 144 + b, 9, stride=16), :] = tile
        return carry

    lax.fori_loop(0, 9, spread_inv, 0)
    loads[5].wait()

    def spread_cpl(ij, carry):
        for b in range(N_GRP):
            tile = cpl_v[ij, :, b * LANES : (b + 1) * LANES].astype(jnp.float32)
            dense[pl.ds(1296 + ij * 16 + b, 3, stride=1296), :] = tile
        return carry

    lax.fori_loop(0, 81, spread_cpl, 0)

    land[g] = own_rhs[...]
    for step in range(1, N_GRP):
        peer = lax.rem(g + step, N_GRP)
        rhs_copy(peer, peer).wait_recv()
    for b in range(N_GRP):
        rhs[pl.ds(b, 9, stride=16), :] = land[b]

    def matrix(base, i, j, h):
        start = (base + i) * 144 + j * 16 + h * 8
        return dense[pl.ds(start if isinstance(h, int) else pl.multiple_of(start, 8), 8), :]

    def apply_inverse(remain, h):
        result = [matrix(0, i, 0, h) * remain[0] for i in range(9)]
        for j in range(1, 9):
            result = [result[i] + matrix(0, i, j, h) * remain[j] for i in range(9)]
        return result

    for h in range(2):
        remain = [rhs[j * 16 + h * 8 : j * 16 + h * 8 + 8, :] for j in range(9)]
        for i, update in enumerate(apply_inverse(remain, h)):
            table[0, i, 16 + 8 * h : 24 + 8 * h, :] = damping * update

    def halo(slot, s, which, h):
        own, there = 16 + 8 * h, (32 if s == 0 else 0) + 8 * h
        return pltpu.make_async_remote_copy(
            src_ref=table.at[slot, :, own : own + 8, :],
            dst_ref=table.at[slot, :, there : there + 8, :],
            send_sem=hsend.at[slot, 4 * s + 2 * which + h],
            recv_sem=hrecv.at[slot, 2 * (1 - s) + h],
            device_id=(side_dom[s], second if which else first[s]),
            device_id_type=MESH,
        )

    def each_send(slot, act):
        for which, flags in ((0, sends), (1, twice)):
            for s in range(2):

                @pl.when(flags[s])
                def _():
                    act(halo(slot, s, which, s))
                    act(halo(slot, s, which, 1 - s))

    each_send(0, lambda copy: copy.start())

    def arrive(slot, s, far):
        for low in range(2):

            @pl.when(jnp.logical_and(s == low, has[low]))
            def _():
                halo(slot, 1 - low, 0, low if far else 1 - low).wait_recv()

    def pick(slot, h, start, k_start, count, resume):
        rows = pl.ds(pl.multiple_of(8 * h, 8), 8)
        for f in range(3):
            lane = lane_idx[f, rows, :]
            block = block_idx[f, rows, :] - k_start
            if resume:
                total = [beside[f * 9 + v, rows, :] for v in range(9)]
            else:
                total = [jnp.zeros((8, LANES), jnp.float32) for v in range(9)]
            for t in range(count):
                mask = block == t
                total = [
                    jnp.where(
                        mask,
                        gathered(table[slot, v, pl.ds(start + t, 8), :], lane),
                        total[v],
                    )
                    for v in range(9)
                ]
            for v in range(9):
                beside[f * 9 + v, rows, :] = total[v]

    def update(slot, h):
        rows = pl.ds(pl.multiple_of(8 * h, 8), 8)
        own = pl.ds(pl.multiple_of(16 + 8 * h, 8), 8)
        total = [jnp.zeros((8, LANES), jnp.float32) for i in range(9)]
        for f in range(3):
            for j in range(9):
                near = beside[f * 9 + j, rows, :]
                total = [total[i] + matrix(9 + 9 * f, i, j, h) * near for i in range(9)]
        remain = [
            rhs[pl.ds(pl.multiple_of(i * 16 + h * 8, 8), 8), :] - total[i] for i in range(9)
        ]
        for i, change in enumerate(apply_inverse(remain, h)):
            now = table[slot, i, own, :]
            table[slot + 1, i, own, :] = (1.0 - damping) * now + damping * change

    early = jnp.where(d < half, 0, 1)
    late = 1 - early

    def sweep(slot, carry):
        for h in range(2):
            pick(slot, h, 16, 16 - 8 * h, 9, False)
        for s in (early, late):
            arrive(slot, s, False)
            for h in range(2):
                pick(slot, h, 8 + 17 * s, 8 + 17 * s - 8 * h, 8, True)
            if s is late:
                update(slot, early)
            arrive(slot, s, True)
            pick(slot, s, 33 * s, 25 * s, 8, True)
        update(slot, late)

        @pl.when(slot < SWEEPS - 2)
        def _():
            each_send(slot + 1, lambda copy: copy.start())

        return carry

    lax.fori_loop(0, SWEEPS - 1, sweep, 0)

    for v in range(3):
        for m in range(3):
            final[m, v : v + 1, :] = table[SWEEPS - 1, 3 * v + m, pl.ds(16 + g, 1), :]
    coarse = [final[m, 0:3, :] for m in range(3)]
    for n in range(15):
        value = sum(pmat_ref[m, n] * coarse[m] for m in range(3))
        for v in range(3):
            out_ref[v, n : n + 1, :] = value[v : v + 1, :]

    for step in range(1, N_GRP):
        peer = lax.rem(g + step, N_GRP)
        rhs_copy(peer, g).wait_send()
    for slot in range(SWEEPS - 1):
        each_send(slot, lambda copy: copy.wait_send())


def solution(mesh):
    n_dom = mesh.shape["dom"]

    def local(
        fine_level_residual,
        restriction_matrix,
        prolongation_matrix,
        block_inverse,
        face_coupling,
        neighbours,
    ):
        width = block_inverse.shape[2]
        call = pl.pallas_call(
            lambda *refs: kernel(n_dom, *refs),
            out_shape=jax.ShapeDtypeStruct((3, 15, LANES), jnp.float32),
            in_specs=[pl.BlockSpec(memory_space=pl.ANY)] * 6,
            out_specs=pl.BlockSpec(memory_space=pltpu.VMEM),
            scratch_shapes=[
                pltpu.VMEM((3, 15, LANES), jnp.float32),
                pltpu.SMEM((3, 15), jnp.float32),
                pltpu.SMEM((3, 15), jnp.float32),
                pltpu.VMEM((3, width), jnp.int32),
                pltpu.VMEM((9, 9, width), jnp.bfloat16),
                pltpu.VMEM((81, 3, width), jnp.bfloat16),
                pltpu.VMEM((36 * 144, LANES), jnp.float32),
                pltpu.VMEM((3, 16, LANES), jnp.int32),
                pltpu.VMEM((3, 16, LANES), jnp.int32),
                pltpu.VMEM((9, LANES), jnp.float32),
                pltpu.VMEM((16, 9, LANES), jnp.float32),
                pltpu.VMEM((144, LANES), jnp.float32),
                pltpu.VMEM((SWEEPS, 9, 48, LANES), jnp.float32),
                pltpu.VMEM((27, 16, LANES), jnp.float32),
                pltpu.VMEM((3, 8, LANES), jnp.float32),
                pltpu.SemaphoreType.DMA((6,)),
                pltpu.SemaphoreType.DMA((16,)),
                pltpu.SemaphoreType.DMA((16,)),
                pltpu.SemaphoreType.DMA((SWEEPS - 1, 8)),
                pltpu.SemaphoreType.DMA((SWEEPS - 1, 4)),
            ],
            compiler_params=pltpu.CompilerParams(collective_id=0, has_side_effects=True),
            name="jacobi",
        )
        return call(
            fine_level_residual,
            restriction_matrix,
            prolongation_matrix.T,
            neighbours,
            block_inverse,
            face_coupling.transpose(1, 2, 0, 3).reshape(81, 3, width),
        )

    placed = (
        P(None, None, ("dom", "grp")),
        P(),
        P(),
        P(None, None, "dom"),
        P(None, None, None, "dom"),
        P(None, "dom"),
    )
    return jax.shard_map(
        local, mesh=mesh, in_specs=placed, out_specs=P(None, None, ("dom", "grp")), check_vma=False
    )
```

time: 58.1 us -> 48.5 us (0.83)
  Pallas kernels: 55.6 us -> 47 us
  other arithmetic: 0.69 us -> 0 us
    pallas_call x1, Pallas kernels: 55.6 us -> 47 us  [local(): call(fine_level_residual, restriction_matrix, prolongation_matrix.T, neig...]
    unnamed x2 -> x1, local copies, waits for them, and re-layouts: 0.01 us -> 1.35 us
    mul x1 -> x0, local copies, waits for them, and re-layouts: 0.8 us -> none  [local(): prolongation_matrix[None, :, m, None] * parts[:, None, m, :]]
    reshape x1 -> x0, local copies, waits for them, and re-layouts: 0.71 us -> none  [local(): parts = iterate.reshape(3, 3, LANES)]
    add x1 -> x0, other arithmetic: 0.69 us -> none  [local(): sum((prolongation_matrix[None, :, m, None] * parts[:, None, m, :] for m i...]
where the time goes in v2:
time: 48.5 us; the launch traced here: 48.3 us
  Pallas kernels  47 us (97%)
  local copies, waits for them, and re-layouts  1.35 us (3%)
    pallas_call x1, Pallas kernels, local(): call(fine_level_residual, restriction_matrix, prolongation_matrix.T, neig...  47 us
    unnamed x1, local copies, waits for them, and re-layouts  1.35 us

profile of v2, /device:TPU:40, one launch (start us, length us, event | category | flops | bytes accessed | tf_op | source)
XLA Modules:
  0.0 48.3 jit_solution(7780618405825312029)
XLA Ops:
  0.0 47.0 %jacobi.1 = f32[3,15,128]{2,1,0:T(8,128)} custom-call(f32[3,15,128]{2,1,0:T(8,128)} %refs_0_.1, f32[3,15]{1,0:T(4,128)} %refs_1_.1, f32[3,15]{1,0:T(4,128)} %bitcast.5, s32[3,2048]{1,0:T(4,128)} %refs_3_.1, bf16[9,9,2048]{2,1,0:T(8,128)(2,1)} %refs_4_.1, bf16[81,3,2048]{2,1,0:T(4,128)(2,1)} %bitcast.4), custom_call_target="tpu_custom_call" | custom-call | tf_op jit(solution)/shard_map/jacobi/pallas_call | solution.py:325
  47.0 1.3 %copy.8 = f32[3,15,128]{2,1,0:T(8,128)} copy(f32[3,15,128]{2,1,0:T(8,128)} %jacobi.1) | data formatting | bytes 46080

commit v3 on v2

--- a/solution.py
+++ b/solution.py
@@ -40,11 +40,15 @@
     table,
     beside,
     final,
+    feed_own,
+    feed,
     load_sem,
     gsend,
     grecv,
     hsend,
     hrecv,
+    fsend,
+    frecv,
 ):
     d = lax.axis_index("dom")
     g = lax.axis_index("grp")
@@ -65,6 +69,8 @@
         jnp.logical_and(has[s], jnp.logical_or(jnp.logical_not(cross[s]), lead)) for s in range(2)
     ]
     twice = [jnp.logical_and(cross[s], lead) for s in range(2)]
+    feeding, fed = cross_high, jnp.logical_and(cross_low, lead)
+    leads = [4 * x + y for x in range(4) for y in (3, 0)]
 
     barrier = pltpu.get_barrier_semaphore()
     for step in range(1, N_GRP):
@@ -72,11 +78,16 @@
         pl.semaphore_signal(barrier, inc=1, device_id=(d, peer), device_id_type=MESH)
     for s in range(2):
 
-        @pl.when(has[s])
+        @pl.when(has[s] if s else jnp.logical_and(has[s], jnp.logical_not(fed)))
         def _():
             pl.semaphore_signal(
                 barrier, inc=1, device_id=(side_dom[s], source[s]), device_id_type=MESH
             )
+
+    @pl.when(fed)
+    def _():
+        for other in range(N_GRP):
+            pl.semaphore_signal(barrier, inc=1, device_id=(d - 1, other), device_id_type=MESH)
 
     loads = [
         pltpu.make_async_copy(src, dst, load_sem.at[i])
@@ -104,8 +115,9 @@
             own_rhs[3 * v + m : 3 * v + m + 1, :] = total[v : v + 1, :]
 
     signals = N_GRP - 1
-    for flag in sends + twice:
+    for flag in [sends[0]] + twice:
         signals = signals + flag.astype(jnp.int32)
+    signals = signals + jnp.where(feeding, len(leads), sends[1].astype(jnp.int32))
     pl.semaphore_wait(barrier, signals)
 
     def rhs_copy(peer, owner):
@@ -121,6 +133,27 @@
     for step in range(1, N_GRP):
         peer = lax.rem(g + step, N_GRP)
         rhs_copy(peer, g).start()
+
+    loads[4].wait()
+
+    def feed_copy(k, owner):
+        return pltpu.make_async_remote_copy(
+            src_ref=feed_own,
+            dst_ref=feed.at[owner],
+            send_sem=fsend.at[k],
+            recv_sem=frecv.at[owner],
+            device_id=(d + 1, leads[k]),
+            device_id_type=MESH,
+        )
+
+    @pl.when(feeding)
+    def _():
+        own = pl.ds(pl.multiple_of(g * LANES, LANES), LANES)
+        for i in range(9):
+            part = inv_v[i, :, own].astype(jnp.float32) * own_rhs[...]
+            feed_own[i : i + 1, :] = damping * jnp.sum(part, axis=0, keepdims=True)
+        for k in range(len(leads)):
+            feed_copy(k, g).start()
 
     loads[2].wait()
     loads[3].wait()
@@ -133,7 +166,6 @@
         block_idx[f] = jnp.where(offsets != 0, lax.shift_right_arithmetic(position, 7), -1)
         lane_idx[f] = jnp.bitwise_and(position, LANES - 1)
 
-    loads[4].wait()
 
     def spread_inv(i, carry):
         for b in range(N_GRP):
@@ -185,11 +217,15 @@
             device_id_type=MESH,
         )
 
-    def each_send(slot, act):
-        for which, flags in ((0, sends), (1, twice)):
+    def each_send(slot, act, inner_first=False):
+        order = ((0, sends), (1, twice))
+        for which, flags in order[::-1] if inner_first else order:
             for s in range(2):
-
-                @pl.when(flags[s])
+                flag = flags[s]
+                if isinstance(slot, int) and slot == 0 and s == 1 and which == 0:
+                    flag = jnp.logical_and(flag, jnp.logical_not(feeding))
+
+                @pl.when(flag)
                 def _():
                     act(halo(slot, s, which, s))
                     act(halo(slot, s, which, 1 - s))
@@ -199,7 +235,11 @@
     def arrive(slot, s, far):
         for low in range(2):
 
-            @pl.when(jnp.logical_and(s == low, has[low]))
+            due = jnp.logical_and(s == low, has[low])
+            if low == 0 and not isinstance(slot, int):
+                due = jnp.logical_and(due, jnp.logical_not(jnp.logical_and(fed, slot == 0)))
+
+            @pl.when(due)
             def _():
                 halo(slot, 1 - low, 0, low if far else 1 - low).wait_recv()
 
@@ -247,6 +287,16 @@
         for h in range(2):
             pick(slot, h, 16, 16 - 8 * h, 9, False)
         for s in (early, late):
+            if s is late:
+
+                @pl.when(jnp.logical_and(fed, slot == 0))
+                def _():
+                    for b in range(N_GRP):
+                        feed_copy(0, b).wait_recv()
+                    for b in range(N_GRP):
+                        for v in range(9):
+                            table[0, v, b : b + 1, :] = feed[b, v : v + 1, :]
+
             arrive(slot, s, False)
             for h in range(2):
                 pick(slot, h, 8 + 17 * s, 8 + 17 * s - 8 * h, 8, True)
@@ -256,18 +306,60 @@
             pick(slot, s, 33 * s, 25 * s, 8, True)
         update(slot, late)
 
-        @pl.when(slot < SWEEPS - 2)
+        @pl.when(slot < SWEEPS - 3)
         def _():
             each_send(slot + 1, lambda copy: copy.start())
 
+        @pl.when(slot == SWEEPS - 3)
+        def _():
+            each_send(slot + 1, lambda copy: copy.start(), True)
+
         return carry
 
-    lax.fori_loop(0, SWEEPS - 1, sweep, 0)
-
-    for v in range(3):
-        for m in range(3):
-            final[m, v : v + 1, :] = table[SWEEPS - 1, 3 * v + m, pl.ds(16 + g, 1), :]
-    coarse = [final[m, 0:3, :] for m in range(3)]
+    lax.fori_loop(0, SWEEPS - 2, sweep, 0)
+
+    last = SWEEPS - 2
+    sublane = lax.broadcasted_iota(jnp.int32, (8, LANES), 0)
+    mine = pl.ds(g, 1)
+
+    def pick_last(tiles, resume):
+        for f in range(3):
+            lane = jnp.broadcast_to(lane_idx[f, mine, :], (8, LANES))
+            block = jnp.broadcast_to(block_idx[f, mine, :], (8, LANES))
+            block = jnp.where(block < 0, -1, block + g - sublane)
+            if resume:
+                total = [beside[f * 9 + v, 0:8, :] for v in range(9)]
+            else:
+                total = [jnp.zeros((8, LANES), jnp.float32) for v in range(9)]
+            for tile in tiles:
+                rows = pl.ds(pl.multiple_of(8 * tile, 8), 8)
+                mask = block == 8 * tile
+                total = [
+                    jnp.where(mask, gathered(table[last, v, rows, :], lane), total[v])
+                    for v in range(9)
+                ]
+            for v in range(9):
+                beside[f * 9 + v, 0:8, :] = total[v]
+
+    pick_last((2, 3), False)
+    for v in range(9):
+        final[0, v : v + 1, :] = table[last, v, pl.ds(16 + g, 1), :]
+    for s in (early, late):
+        arrive(last, s, False)
+        pick_last((1 + 3 * s,), True)
+        arrive(last, s, True)
+        pick_last((5 * s,), True)
+    coupled = jnp.zeros((9, LANES), jnp.float32)
+    for f in range(3):
+        for j in range(9):
+            near = jnp.sum(beside[f * 9 + j, 0:8, :], axis=0, keepdims=True)
+            coupled = coupled + dense[pl.ds((9 + 9 * f) * 144 + j * 16 + g, 9, stride=144), :] * near
+    final[1, 0:9, :] = rhs[pl.ds(g, 9, stride=16), :] - coupled
+    change = jnp.zeros((9, LANES), jnp.float32)
+    for j in range(9):
+        change = change + dense[pl.ds(j * 16 + g, 9, stride=144), :] * final[1, j : j + 1, :]
+    final[2, 0:9, :] = (1.0 - damping) * final[0, 0:9, :] + damping * change
+    coarse = [final[2, pl.ds(m, 3, stride=3), :] for m in range(3)]
     for n in range(15):
         value = sum(pmat_ref[m, n] * coarse[m] for m in range(3))
         for v in range(3):
@@ -278,6 +370,11 @@
         rhs_copy(peer, g).wait_send()
     for slot in range(SWEEPS - 1):
         each_send(slot, lambda copy: copy.wait_send())
+
+    @pl.when(feeding)
+    def _():
+        for k in range(len(leads)):
+            feed_copy(k, g).wait_send()
 
 
 def solution(mesh):
@@ -310,14 +407,18 @@
                 pltpu.VMEM((9, LANES), jnp.float32),
                 pltpu.VMEM((16, 9, LANES), jnp.float32),
                 pltpu.VMEM((144, LANES), jnp.float32),
-                pltpu.VMEM((SWEEPS, 9, 48, LANES), jnp.float32),
+                pltpu.VMEM((SWEEPS - 1, 9, 48, LANES), jnp.float32),
                 pltpu.VMEM((27, 16, LANES), jnp.float32),
-                pltpu.VMEM((3, 8, LANES), jnp.float32),
+                pltpu.VMEM((3, 16, LANES), jnp.float32),
+                pltpu.VMEM((9, LANES), jnp.float32),
+                pltpu.VMEM((16, 9, LANES), jnp.float32),
                 pltpu.SemaphoreType.DMA((6,)),
                 pltpu.SemaphoreType.DMA((16,)),
                 pltpu.SemaphoreType.DMA((16,)),
                 pltpu.SemaphoreType.DMA((SWEEPS - 1, 8)),
                 pltpu.SemaphoreType.DMA((SWEEPS - 1, 4)),
+                pltpu.SemaphoreType.DMA((8,)),
+                pltpu.SemaphoreType.DMA((16,)),
             ],
             compiler_params=pltpu.CompilerParams(collective_id=0, has_side_effects=True),
             name="jacobi",

time: 48.5 us -> 47.3 us (0.975)
  the two profiles are of different devices: /device:TPU:40 before, /device:TPU:56 now
where the time goes in v3:
time: 47.3 us; the launch traced here: 47 us
  Pallas kernels  45.7 us (97%)
  local copies, waits for them, and re-layouts  1.35 us (3%)
    pallas_call x1, Pallas kernels, local(): call(fine_level_residual, restriction_matrix, prolongation_matrix.T, neig...  45.7 us
    unnamed x1, local copies, waits for them, and re-layouts  1.35 us

profile of v3, /device:TPU:56, one launch (start us, length us, event | category | flops | bytes accessed | tf_op | source)
XLA Modules:
  0.0 47.0 jit_solution(8546120897275352605)
XLA Ops:
  0.0 45.7 %jacobi.1 = f32[3,15,128]{2,1,0:T(8,128)} custom-call(f32[3,15,128]{2,1,0:T(8,128)} %refs_0_.1, f32[3,15]{1,0:T(4,128)} %refs_1_.1, f32[3,15]{1,0:T(4,128)} %bitcast.5, s32[3,2048]{1,0:T(4,128)} %refs_3_.1, bf16[9,9,2048]{2,1,0:T(8,128)(2,1)} %refs_4_.1, bf16[81,3,2048]{2,1,0:T(4,128)(2,1)} %bitcast.4), custom_call_target="tpu_custom_call" | custom-call | tf_op jit(solution)/shard_map/jacobi/pallas_call | solution.py:426
  45.7 1.3 %copy.8 = f32[3,15,128]{2,1,0:T(8,128)} copy(f32[3,15,128]{2,1,0:T(8,128)} %jacobi.1) | data formatting | bytes 46080

commit v4 on v3

--- a/solution.py
+++ b/solution.py
@@ -49,6 +49,7 @@
     hrecv,
     fsend,
     frecv,
+    ready,
 ):
     d = lax.axis_index("dom")
     g = lax.axis_index("grp")
@@ -78,7 +79,7 @@
         pl.semaphore_signal(barrier, inc=1, device_id=(d, peer), device_id_type=MESH)
     for s in range(2):
 
-        @pl.when(has[s] if s else jnp.logical_and(has[s], jnp.logical_not(fed)))
+        @pl.when(jnp.logical_and(has[s], jnp.logical_not(feeding if s else fed)))
         def _():
             pl.semaphore_signal(
                 barrier, inc=1, device_id=(side_dom[s], source[s]), device_id_type=MESH
@@ -115,10 +116,16 @@
             own_rhs[3 * v + m : 3 * v + m + 1, :] = total[v : v + 1, :]
 
     signals = N_GRP - 1
-    for flag in [sends[0]] + twice:
-        signals = signals + flag.astype(jnp.int32)
+    low = jnp.logical_and(sends[0], jnp.logical_not(cross_low))
+    signals = signals + low.astype(jnp.int32) + twice[1].astype(jnp.int32)
     signals = signals + jnp.where(feeding, len(leads), sends[1].astype(jnp.int32))
     pl.semaphore_wait(barrier, signals)
+
+    @pl.when(feeding)
+    def _():
+        pl.semaphore_signal(
+            ready, inc=1, device_id=(side_dom[1], source[1]), device_id_type=MESH
+        )
 
     def rhs_copy(peer, owner):
         return pltpu.make_async_remote_copy(
@@ -217,10 +224,10 @@
             device_id_type=MESH,
         )
 
-    def each_send(slot, act, inner_first=False):
+    def each_send(slot, act, inner_first=False, sides=(0, 1)):
         order = ((0, sends), (1, twice))
         for which, flags in order[::-1] if inner_first else order:
-            for s in range(2):
+            for s in sides:
                 flag = flags[s]
                 if isinstance(slot, int) and slot == 0 and s == 1 and which == 0:
                     flag = jnp.logical_and(flag, jnp.logical_not(feeding))
@@ -230,7 +237,13 @@
                     act(halo(slot, s, which, s))
                     act(halo(slot, s, which, 1 - s))
 
-    each_send(0, lambda copy: copy.start())
+    each_send(0, lambda copy: copy.start(), sides=(1,))
+
+    @pl.when(fed)
+    def _():
+        pl.semaphore_wait(ready, 2)
+
+    each_send(0, lambda copy: copy.start(), sides=(0,))
 
     def arrive(slot, s, far):
         for low in range(2):
@@ -419,6 +432,7 @@
                 pltpu.SemaphoreType.DMA((SWEEPS - 1, 4)),
                 pltpu.SemaphoreType.DMA((8,)),
                 pltpu.SemaphoreType.DMA((16,)),
+                pltpu.SemaphoreType.REGULAR,
             ],
             compiler_params=pltpu.CompilerParams(collective_id=0, has_side_effects=True),
             name="jacobi",

time: 47.3 us -> 45.7 us (0.966)
  Pallas kernels: 45.7 us -> 44.1 us
    pallas_call x1, Pallas kernels: 45.7 us -> 44.1 us  [local(): call(fine_level_residual, restriction_matrix, prolongation_matrix.T, neig...]
where the time goes in v4:
time: 45.7 us; the launch traced here: 45.5 us
  Pallas kernels  44.1 us (96%)
  local copies, waits for them, and re-layouts  1.35 us (3%)
    pallas_call x1, Pallas kernels, local(): call(fine_level_residual, restriction_matrix, prolongation_matrix.T, neig...  44.1 us
    unnamed x1, local copies, waits for them, and re-layouts  1.35 us

profile of v4, /device:TPU:56, one launch (start us, length us, event | category | flops | bytes accessed | tf_op | source)
XLA Modules:
  0.0 45.5 jit_solution(17023236906843644588)
XLA Ops:
  0.0 44.1 %jacobi.1 = f32[3,15,128]{2,1,0:T(8,128)} custom-call(f32[3,15,128]{2,1,0:T(8,128)} %refs_0_.1, f32[3,15]{1,0:T(4,128)} %refs_1_.1, f32[3,15]{1,0:T(4,128)} %bitcast.5, s32[3,2048]{1,0:T(4,128)} %refs_3_.1, bf16[9,9,2048]{2,1,0:T(8,128)(2,1)} %refs_4_.1, bf16[81,3,2048]{2,1,0:T(4,128)(2,1)} %bitcast.4), custom_call_target="tpu_custom_call" | custom-call | tf_op jit(solution)/shard_map/jacobi/pallas_call | solution.py:440
  44.1 1.3 %copy.8 = f32[3,15,128]{2,1,0:T(8,128)} copy(f32[3,15,128]{2,1,0:T(8,128)} %jacobi.1) | data formatting | bytes 46080

commit v5 on v4

--- a/solution.py
+++ b/solution.py
@@ -50,6 +50,8 @@
     fsend,
     frecv,
     ready,
+    ready_high,
+    group_ready,
 ):
     d = lax.axis_index("dom")
     g = lax.axis_index("grp")
@@ -73,23 +75,6 @@
     feeding, fed = cross_high, jnp.logical_and(cross_low, lead)
     leads = [4 * x + y for x in range(4) for y in (3, 0)]
 
-    barrier = pltpu.get_barrier_semaphore()
-    for step in range(1, N_GRP):
-        peer = lax.rem(g + step, N_GRP)
-        pl.semaphore_signal(barrier, inc=1, device_id=(d, peer), device_id_type=MESH)
-    for s in range(2):
-
-        @pl.when(jnp.logical_and(has[s], jnp.logical_not(feeding if s else fed)))
-        def _():
-            pl.semaphore_signal(
-                barrier, inc=1, device_id=(side_dom[s], source[s]), device_id_type=MESH
-            )
-
-    @pl.when(fed)
-    def _():
-        for other in range(N_GRP):
-            pl.semaphore_signal(barrier, inc=1, device_id=(d - 1, other), device_id_type=MESH)
-
     loads = [
         pltpu.make_async_copy(src, dst, load_sem.at[i])
         for i, (src, dst) in enumerate(
@@ -106,6 +91,52 @@
     for load in loads:
         load.start()
 
+    early = jnp.where(d < half, 0, 1)
+    late = 1 - early
+    barrier = pltpu.get_barrier_semaphore()
+    order = [0, 4, 1, 12, 8, 5, 2, 13, 9, 6, 3, 14, 10, 7, 15, 11]
+    rank = sum(jnp.where(g == device, k, 0) for k, device in enumerate(order))
+
+    for k, peer in enumerate(order):
+
+        @pl.when(jnp.where(feeding, k > rank, k != rank))
+        def _():
+            pl.semaphore_signal(barrier, inc=1, device_id=(d, peer), device_id_type=MESH)
+    answers_low = d == half + 1
+    for s in range(2):
+        silent = feeding if s else jnp.logical_or(fed, answers_low)
+
+        @pl.when(jnp.logical_and(has[s], jnp.logical_not(silent)))
+        def _():
+            pl.semaphore_signal(
+                barrier, inc=1, device_id=(side_dom[s], source[s]), device_id_type=MESH
+            )
+
+    @pl.when(fed)
+    def _():
+        for other in range(N_GRP):
+            pl.semaphore_signal(barrier, inc=1, device_id=(d - 1, other), device_id_type=MESH)
+
+    low = jnp.logical_and(sends[0], jnp.logical_not(cross_low))
+    high = jnp.logical_and(sends[1], jnp.logical_not(cross_low))
+    signals = jnp.where(feeding, rank + len(leads), N_GRP - 1 + high.astype(jnp.int32))
+    signals = signals + low.astype(jnp.int32) + twice[1].astype(jnp.int32)
+
+    @pl.when(feeding)
+    def _():
+        pl.semaphore_wait(barrier, signals)
+        for k, peer in enumerate(order):
+
+            @pl.when(k < rank)
+            def _():
+                pl.semaphore_signal(
+                    group_ready, inc=1, device_id=(d, peer), device_id_type=MESH
+                )
+
+        pl.semaphore_signal(
+            ready, inc=1, device_id=(side_dom[1], source[1]), device_id_type=MESH
+        )
+
     loads[0].wait()
     loads[1].wait()
     for m in range(3):
@@ -115,17 +146,13 @@
         for v in range(3):
             own_rhs[3 * v + m : 3 * v + m + 1, :] = total[v : v + 1, :]
 
-    signals = N_GRP - 1
-    low = jnp.logical_and(sends[0], jnp.logical_not(cross_low))
-    signals = signals + low.astype(jnp.int32) + twice[1].astype(jnp.int32)
-    signals = signals + jnp.where(feeding, len(leads), sends[1].astype(jnp.int32))
-    pl.semaphore_wait(barrier, signals)
-
-    @pl.when(feeding)
-    def _():
-        pl.semaphore_signal(
-            ready, inc=1, device_id=(side_dom[1], source[1]), device_id_type=MESH
-        )
+    @pl.when(jnp.logical_not(feeding))
+    def _():
+        pl.semaphore_wait(barrier, signals)
+
+    @pl.when(answers_low)
+    def _():
+        pl.semaphore_signal(ready_high, inc=1, device_id=(d - 1, g), device_id_type=MESH)
 
     def rhs_copy(peer, owner):
         return pltpu.make_async_remote_copy(
@@ -137,12 +164,6 @@
             device_id_type=MESH,
         )
 
-    for step in range(1, N_GRP):
-        peer = lax.rem(g + step, N_GRP)
-        rhs_copy(peer, g).start()
-
-    loads[4].wait()
-
     def feed_copy(k, owner):
         return pltpu.make_async_remote_copy(
             src_ref=feed_own,
@@ -155,12 +176,21 @@
 
     @pl.when(feeding)
     def _():
+        loads[4].wait()
         own = pl.ds(pl.multiple_of(g * LANES, LANES), LANES)
         for i in range(9):
             part = inv_v[i, :, own].astype(jnp.float32) * own_rhs[...]
             feed_own[i : i + 1, :] = damping * jnp.sum(part, axis=0, keepdims=True)
         for k in range(len(leads)):
             feed_copy(k, g).start()
+
+    @pl.when(jnp.logical_and(feeding, rank < N_GRP - 1))
+    def _():
+        pl.semaphore_wait(group_ready, N_GRP - 1 - rank)
+
+    for step in range(1, N_GRP):
+        peer = lax.rem(g + step, N_GRP)
+        rhs_copy(peer, g).start()
 
     loads[2].wait()
     loads[3].wait()
@@ -173,6 +203,10 @@
         block_idx[f] = jnp.where(offsets != 0, lax.shift_right_arithmetic(position, 7), -1)
         lane_idx[f] = jnp.bitwise_and(position, LANES - 1)
 
+    @pl.when(jnp.logical_not(feeding))
+    def _():
+        loads[4].wait()
+
 
     def spread_inv(i, carry):
         for b in range(N_GRP):
@@ -224,9 +258,8 @@
             device_id_type=MESH,
         )
 
-    def each_send(slot, act, inner_first=False, sides=(0, 1)):
-        order = ((0, sends), (1, twice))
-        for which, flags in order[::-1] if inner_first else order:
+    def each_send(slot, act, sides=(0, 1)):
+        for which, flags in ((0, sends), (1, twice)):
             for s in sides:
                 flag = flags[s]
                 if isinstance(slot, int) and slot == 0 and s == 1 and which == 0:
@@ -237,13 +270,43 @@
                     act(halo(slot, s, which, s))
                     act(halo(slot, s, which, 1 - s))
 
+    @pl.when(fed)
+    def _():
+        pl.semaphore_wait(ready, 2)
+
+    each_send(0, lambda copy: copy.start(), sides=(0,))
+
+    @pl.when(cross_low)
+    def _():
+        pl.semaphore_wait(ready_high, 1)
+
     each_send(0, lambda copy: copy.start(), sides=(1,))
 
-    @pl.when(fed)
-    def _():
-        pl.semaphore_wait(ready, 2)
-
-    each_send(0, lambda copy: copy.start(), sides=(0,))
+    def send_half(slot, part):
+        for s in range(2):
+
+            @pl.when(jnp.logical_and(late == s, jnp.logical_and(twice[s], slot == SWEEPS - 2)))
+            def _():
+                halo(slot, s, 1, 1 - s if part else s).start()
+
+            @pl.when(jnp.logical_and(late == s, sends[s]))
+            def _():
+                halo(slot, s, 0, 1 - s if part else s).start()
+
+        if part:
+            for s in range(2):
+
+                @pl.when(jnp.logical_and(early == s, sends[s]))
+                def _():
+                    halo(slot, s, 0, s).start()
+                    halo(slot, s, 0, 1 - s).start()
+
+            for s in range(2):
+
+                @pl.when(jnp.logical_and(late == s, jnp.logical_and(twice[s], slot < SWEEPS - 2)))
+                def _():
+                    halo(slot, s, 1, s).start()
+                    halo(slot, s, 1, 1 - s).start()
 
     def arrive(slot, s, far):
         for low in range(2):
@@ -293,40 +356,32 @@
             now = table[slot, i, own, :]
             table[slot + 1, i, own, :] = (1.0 - damping) * now + damping * change
 
-    early = jnp.where(d < half, 0, 1)
-    late = 1 - early
-
     def sweep(slot, carry):
         for h in range(2):
             pick(slot, h, 16, 16 - 8 * h, 9, False)
-        for s in (early, late):
-            if s is late:
-
-                @pl.when(jnp.logical_and(fed, slot == 0))
-                def _():
-                    for b in range(N_GRP):
-                        feed_copy(0, b).wait_recv()
-                    for b in range(N_GRP):
-                        for v in range(9):
-                            table[0, v, b : b + 1, :] = feed[b, v : v + 1, :]
-
-            arrive(slot, s, False)
-            for h in range(2):
-                pick(slot, h, 8 + 17 * s, 8 + 17 * s - 8 * h, 8, True)
-            if s is late:
-                update(slot, early)
-            arrive(slot, s, True)
-            pick(slot, s, 33 * s, 25 * s, 8, True)
+        arrive(slot, early, False)
+        for h in range(2):
+            pick(slot, h, 8 + 17 * early, 8 + 17 * early - 8 * h, 8, True)
+        arrive(slot, early, True)
+        pick(slot, early, 33 * early, 25 * early, 8, True)
+
+        @pl.when(jnp.logical_and(fed, slot == 0))
+        def _():
+            for b in range(N_GRP):
+                feed_copy(0, b).wait_recv()
+            for b in range(N_GRP):
+                for v in range(9):
+                    table[0, v, b : b + 1, :] = feed[b, v : v + 1, :]
+
+        arrive(slot, late, False)
+        pick(slot, late, 8 + 17 * late, 8 + 9 * late, 8, True)
+        arrive(slot, late, True)
+        pick(slot, late, 33 * late, 25 * late, 8, True)
         update(slot, late)
-
-        @pl.when(slot < SWEEPS - 3)
-        def _():
-            each_send(slot + 1, lambda copy: copy.start())
-
-        @pl.when(slot == SWEEPS - 3)
-        def _():
-            each_send(slot + 1, lambda copy: copy.start(), True)
-
+        send_half(slot + 1, 0)
+        pick(slot, early, 8 + 17 * late, 25 * late, 8, True)
+        update(slot, early)
+        send_half(slot + 1, 1)
         return carry
 
     lax.fori_loop(0, SWEEPS - 2, sweep, 0)
@@ -433,6 +488,8 @@
                 pltpu.SemaphoreType.DMA((8,)),
                 pltpu.SemaphoreType.DMA((16,)),
                 pltpu.SemaphoreType.REGULAR,
+                pltpu.SemaphoreType.REGULAR,
+                pltpu.SemaphoreType.REGULAR,
             ],
             compiler_params=pltpu.CompilerParams(collective_id=0, has_side_effects=True),
             name="jacobi",

time: 45.7 us -> 44.5 us (0.974)
  Pallas kernels: 44.1 us -> 42.9 us
    pallas_call x1, Pallas kernels: 44.1 us -> 42.9 us  [local(): call(fine_level_residual, restriction_matrix, prolongation_matrix.T, neig...]
where the time goes in v5:
time: 44.5 us; the launch traced here: 44.3 us
  Pallas kernels  42.9 us (96%)
  local copies, waits for them, and re-layouts  1.35 us (3%)
    pallas_call x1, Pallas kernels, local(): call(fine_level_residual, restriction_matrix, prolongation_matrix.T, neig...  42.9 us
    unnamed x1, local copies, waits for them, and re-layouts  1.35 us

profile of v5, /device:TPU:56, one launch (start us, length us, event | category | flops | bytes accessed | tf_op | source)
XLA Modules:
  0.0 44.3 jit_solution(16867818501646868295)
XLA Ops:
  0.0 42.9 %jacobi.1 = f32[3,15,128]{2,1,0:T(8,128)} custom-call(f32[3,15,128]{2,1,0:T(8,128)} %refs_0_.1, f32[3,15]{1,0:T(4,128)} %refs_1_.1, f32[3,15]{1,0:T(4,128)} %bitcast.5, s32[3,2048]{1,0:T(4,128)} %refs_3_.1, bf16[9,9,2048]{2,1,0:T(8,128)(2,1)} %refs_4_.1, bf16[81,3,2048]{2,1,0:T(4,128)(2,1)} %bitcast.4), custom_call_target="tpu_custom_call" | custom-call | tf_op jit(solution)/shard_map/jacobi/pallas_call | solution.py:497
  42.9 1.3 %copy.8 = f32[3,15,128]{2,1,0:T(8,128)} copy(f32[3,15,128]{2,1,0:T(8,128)} %jacobi.1) | data formatting | bytes 46080

commit v6 on v5

--- a/solution.py
+++ b/solution.py
@@ -359,22 +359,28 @@
     def sweep(slot, carry):
         for h in range(2):
             pick(slot, h, 16, 16 - 8 * h, 9, False)
+        fresh = jnp.logical_and(fed, slot == 0)
+
+        @pl.when(fresh)
+        def _():
+            for b in order:
+                feed_copy(0, b).wait_recv()
+                for v in range(9):
+                    table[0, v, b : b + 1, :] = feed[b, v : v + 1, :]
+            pick(slot, late, 8 + 17 * late, 8 + 9 * late, 8, True)
+
         arrive(slot, early, False)
         for h in range(2):
             pick(slot, h, 8 + 17 * early, 8 + 17 * early - 8 * h, 8, True)
         arrive(slot, early, True)
         pick(slot, early, 33 * early, 25 * early, 8, True)
 
-        @pl.when(jnp.logical_and(fed, slot == 0))
+        arrive(slot, late, False)
+
+        @pl.when(jnp.logical_not(fresh))
         def _():
-            for b in range(N_GRP):
-                feed_copy(0, b).wait_recv()
-            for b in range(N_GRP):
-                for v in range(9):
-                    table[0, v, b : b + 1, :] = feed[b, v : v + 1, :]
-
-        arrive(slot, late, False)
-        pick(slot, late, 8 + 17 * late, 8 + 9 * late, 8, True)
+            pick(slot, late, 8 + 17 * late, 8 + 9 * late, 8, True)
+
         arrive(slot, late, True)
         pick(slot, late, 33 * late, 25 * late, 8, True)
         update(slot, late)

time: 44.5 us -> 45.3 us (1.018)
  Pallas kernels: 42.9 us -> 43.7 us
    pallas_call x1, Pallas kernels: 42.9 us -> 43.7 us  [local(): call(fine_level_residual, restriction_matrix, prolongation_matrix.T, neig...]
where the time goes in v6:
time: 45.3 us; the launch traced here: 45.1 us
  Pallas kernels  43.7 us (96%)
  local copies, waits for them, and re-layouts  1.35 us (3%)
    pallas_call x1, Pallas kernels, local(): call(fine_level_residual, restriction_matrix, prolongation_matrix.T, neig...  43.7 us
    unnamed x1, local copies, waits for them, and re-layouts  1.35 us

profile of v6, /device:TPU:56, one launch (start us, length us, event | category | flops | bytes accessed | tf_op | source)
XLA Modules:
  0.0 45.1 jit_solution(11604735799989585129)
XLA Ops:
  0.0 43.7 %jacobi.1 = f32[3,15,128]{2,1,0:T(8,128)} custom-call(f32[3,15,128]{2,1,0:T(8,128)} %refs_0_.1, f32[3,15]{1,0:T(4,128)} %refs_1_.1, f32[3,15]{1,0:T(4,128)} %bitcast.5, s32[3,2048]{1,0:T(4,128)} %refs_3_.1, bf16[9,9,2048]{2,1,0:T(8,128)(2,1)} %refs_4_.1, bf16[81,3,2048]{2,1,0:T(4,128)(2,1)} %bitcast.4), custom_call_target="tpu_custom_call" | custom-call | tf_op jit(solution)/shard_map/jacobi/pallas_call | solution.py:503
  43.8 1.3 %copy.8 = f32[3,15,128]{2,1,0:T(8,128)} copy(f32[3,15,128]{2,1,0:T(8,128)} %jacobi.1) | data formatting | bytes 46080
